TPU v7x, 32 devices: a whole 2x2x4 slice. The times are simulated.
32 devices in a mesh: wide: 16 (over z, y, x), narrow: 2 (over core).
Axes of the slice: x: 2, y: 2, z: 4, core: 2. Of those that a mesh axis runs over, the one named last changes fastest.
Arguments:
- inputs: float32 [16, 64, 16, 128], P(None, 'wide', 'narrow'), may hold values from -100 to 100
- old_basis: float32 [256, 64, 16, 128], P(None, 'wide', 'narrow'), may hold values from -12 to 12
- conductance: float32 [64, 16, 128], P('wide', 'narrow'), may hold values from 0.5 to 2
- shifts: float32 [3], replicated, may hold values from 0.2 to 4
Outputs:
- new_columns: float32 [48, 64, 16, 128], P(None, 'wide', 'narrow')
- coefficients: float32 [256, 48], replicated
- col_scale: float32 [48], replicated
All inputs are finite; a program needn't handle non-finite values.
Results may differ from a plain program's by a relative error of at most 0.00011.
Values sent between devices are 32-bit elements; how exact they have to be, the bound alone decides.
No kernel may reach another device: no remote copies, remote signals or barrier semaphores. Data moves between devices by JAX's collectives and lax.ppermute only.
A program may use at most 64 MiB of HBM per device.

v0:
```python
import jax
import jax.numpy as jnp
from jax import lax
from jax.sharding import PartitionSpec as P

ITERS = 4


def padded_2(cells, sides, width):
    for axis, dim in sides:
        count = lax.axis_size(axis)
        ends = count - 1
        head = lax.slice_in_dim(cells, 0, width, axis=dim)
        tail = lax.slice_in_dim(cells, cells.shape[dim] - width, cells.shape[dim], axis=dim)
        cells = jnp.concatenate(
            [
                lax.ppermute(tail, axis, [(i, (i + 1) % count) for i in range(ends)]),
                cells,
                lax.ppermute(head, axis, [((i + 1) % count, i) for i in range(ends)]),
            ],
            axis=dim,
        )
    return cells


def spread(coef):
    return coef[:, None, None, None]


def stencil(padded, conductance, shift_col):
    center = padded[:, 1:-1, 1:-1, :]
    deeper = jnp.pad(padded, ((0, 0), (0, 0), (0, 0), (1, 1)))
    beside_all = deeper[:, 2:, 1:-1, 1:-1] + deeper[:, :-2, 1:-1, 1:-1]
    beside_all = beside_all + deeper[:, 1:-1, 2:, 1:-1] + deeper[:, 1:-1, :-2, 1:-1]
    beside_all = beside_all + deeper[:, 1:-1, 1:-1, 2:] + deeper[:, 1:-1, 1:-1, :-2]
    return conductance[None] * (6.0 * center - beside_all) + spread(shift_col) * center


def operate(values, conductance, shift_col):
    padded = padded_2(values, (("wide", 1), ("narrow", 2)), 1)
    return stencil(padded, conductance, shift_col)


def local_dot(left, right):
    return jnp.sum(left * right, axis=(1, 2, 3))


def shards(inputs, old_basis, conductance, shifts):
    total_cells = (
        inputs.shape[1]
        * inputs.shape[2]
        * inputs.shape[3]
        * lax.axis_size("wide")
        * lax.axis_size("narrow")
    )
    shift_col = jnp.repeat(shifts, inputs.shape[0])
    shadow = jnp.tile(inputs, (shifts.shape[0], 1, 1, 1))
    columns = shadow.shape[0]
    solution = jnp.zeros_like(shadow)
    residual = shadow
    search = shadow
    rho_now = lax.psum(local_dot(shadow, shadow), ("wide", "narrow")) / total_cells
    for iteration in range(ITERS):
        search_image = operate(search, conductance, shift_col)
        denominator = lax.psum(local_dot(shadow, search_image), ("wide", "narrow")) / total_cells
        step_alpha = rho_now / denominator
        halfway = residual - spread(step_alpha) * search_image
        halfway_image = operate(halfway, conductance, shift_col)
        cross_sum, square_sum, shadow_half, shadow_image = lax.psum(
            (
                local_dot(halfway_image, halfway),
                local_dot(halfway_image, halfway_image),
                local_dot(shadow, halfway),
                local_dot(shadow, halfway_image),
            ),
            ("wide", "narrow"),
        )
        step_omega = cross_sum / total_cells / (square_sum / total_cells + 1e-06)
        solution = solution + spread(step_alpha) * search + spread(step_omega) * halfway
        residual = halfway - spread(step_omega) * halfway_image
        rho_next = shadow_half / total_cells - step_omega * (shadow_image / total_cells)
        if iteration + 1 < ITERS:
            step_beta = rho_next / rho_now * (step_alpha / step_omega)
            search = residual + spread(step_beta) * (search - spread(step_omega) * search_image)
            rho_now = rho_next
    vflat = old_basis.reshape(old_basis.shape[0], -1)
    wflat = solution.reshape(columns, -1)
    high = lax.Precision.HIGHEST
    first_coef = (
        lax.psum(jnp.einsum("bc,kc->bk", vflat, wflat, precision=high), ("wide", "narrow"))
        / total_cells
    )
    once = wflat - jnp.einsum("bk,bc->kc", first_coef, vflat, precision=high)
    second_coef = (
        lax.psum(jnp.einsum("bc,kc->bk", vflat, once, precision=high), ("wide", "narrow"))
        / total_cells
    )
    twice = once - jnp.einsum("bk,bc->kc", second_coef, vflat, precision=high)
    mean_square = lax.psum(jnp.sum(twice * twice, axis=1), ("wide", "narrow")) / total_cells
    col_scale = jnp.sqrt(mean_square + 1e-06)
    new_columns = (twice / col_scale[:, None]).reshape(solution.shape)
    return (new_columns, first_coef + second_coef, col_scale)


def solution(mesh):
    in_specs = (
        P(None, "wide", "narrow", None),
        P(None, "wide", "narrow", None),
        P("wide", "narrow", None),
        P(),
    )
    out_specs = (P(None, "wide", "narrow", None), P(), P())
    return jax.shard_map(shards, mesh=mesh, in_specs=in_specs, out_specs=out_specs, check_vma=False)
```

profile of v0, /device:TPU:0, one launch (start us, length us, event | category | flops | bytes accessed | tf_op | source)
XLA Modules:
  0.0 634.8 jit_solution(9891462262970364943)
XLA Ops:
  1.9 4.9 collective-permute-start.1
  8.1 2.8 collective-permute-done.1
  10.9 6.2 collective-permute-done
  23.1 40.2 %all-reduce.12 = (f32[48]{0:T(128)S(1)}, f32[48]{0:T(128)S(1)}) all-reduce(f32[48]{0:T(128)S(1)} %get-tuple-element.50, f32[48]{0:T(128)S(1)} %reduce_sum.183), channel_id=1, replica_groups=mesh['wide'=16,'narrow'=2] {'wide','narrow'}, use_global_device_ids=true, to_apply=%region_3.4 | all-reduce | flops 96 | bytes 768 | tf_op jit(solution)/shard_map/psum | solution.py:65
  63.5 4.2 collective-permute-start.5
  69.0 6.1 collective-permute-done.5
  83.2 39.4 %all-reduce.11 = (f32[48]{0:T(128)S(1)}, f32[48]{0:T(128)S(1)}, f32[48]{0:T(128)S(1)}, f32[48]{0:T(128)S(1)}) all-reduce(f32[48]{0:T(128)S(1)} %get-tuple-element.4, f32[48]{0:T(128)S(1)} %get-tuple-element.6, f32[48]{0:T(128)S(1)} %get-tuple-element.5, ...), channel_id=1, replica_groups=mesh['wide'=16,'narrow'=2] {'wide','narrow'}, use_global_device_ids=true, to_apply=%region_5.6 | all-reduce | flops 192 | bytes 1536 | tf_op jit(solution)/shard_map/psum | solution.py:69
  122.9 4.2 collective-permute-start.9
  128.4 6.1 collective-permute-done.9
  142.4 38.4 %psum.160 = f32[48]{0:T(128)S(1)} all-reduce(f32[48]{0:T(128)S(1)} %get-tuple-element.44), channel_id=1, replica_groups=mesh['wide'=16,'narrow'=2] {'wide','narrow'}, use_global_device_ids=true, to_apply=%region_13.14 | all-reduce | flops 48 | bytes 384 | tf_op jit(solution)/shard_map/psum | solution.py:65
  182.2 4.2 collective-permute-start.13
  189.5 5.9 collective-permute-done.12
  202.5 39.3 %all-reduce.10 = (f32[48]{0:T(128)S(1)}, f32[48]{0:T(128)S(1)}, f32[48]{0:T(128)S(1)}, f32[48]{0:T(128)S(1)}) all-reduce(f32[48]{0:T(128)S(1)} %get-tuple-element.14, f32[48]{0:T(128)S(1)} %get-tuple-element.16, f32[48]{0:T(128)S(1)} %get-tuple-element.15, ...), channel_id=1, replica_groups=mesh['wide'=16,'narrow'=2] {'wide','narrow'}, use_global_device_ids=true, to_apply=%region_15.16 | all-reduce | flops 192 | bytes 1536 | tf_op jit(solution)/shard_map/psum | solution.py:69
  243.3 4.2 collective-permute-start.17
  248.8 6.1 collective-permute-done.17
  263.6 38.4 %psum.165 = f32[48]{0:T(128)S(1)} all-reduce(f32[48]{0:T(128)S(1)} %get-tuple-element.38), channel_id=1, replica_groups=mesh['wide'=16,'narrow'=2] {'wide','narrow'}, use_global_device_ids=true, to_apply=%region_23.24 | all-reduce | flops 48 | bytes 384 | tf_op jit(solution)/shard_map/psum | solution.py:65
  303.6 4.2 collective-permute-start.21
  310.9 5.9 collective-permute-done.20
  323.9 39.3 %all-reduce.9 = (f32[48]{0:T(128)S(1)}, f32[48]{0:T(128)S(1)}, f32[48]{0:T(128)S(1)}, f32[48]{0:T(128)S(1)}) all-reduce(f32[48]{0:T(128)S(1)} %get-tuple-element.10, f32[48]{0:T(128)S(1)} %get-tuple-element.12, f32[48]{0:T(128)S(1)} %get-tuple-element.11, ...), channel_id=1, replica_groups=mesh['wide'=16,'narrow'=2] {'wide','narrow'}, use_global_device_ids=true, to_apply=%region_25.26 | all-reduce | flops 192 | bytes 1536 | tf_op jit(solution)/shard_map/psum | solution.py:69
  364.9 4.2 collective-permute-start.25
  370.4 6.1 collective-permute-done.25
  385.2 38.4 %psum.170 = f32[48]{0:T(128)S(1)} all-reduce(f32[48]{0:T(128)S(1)} %get-tuple-element.33), channel_id=1, replica_groups=mesh['wide'=16,'narrow'=2] {'wide','narrow'}, use_global_device_ids=true, to_apply=%region_33.34 | all-reduce | flops 48 | bytes 384 | tf_op jit(solution)/shard_map/psum | solution.py:65
  425.2 4.2 collective-permute-start.29
  432.6 5.9 collective-permute-done.28
  444.5 39.3 %all-reduce.8 = (f32[48]{0:T(128)S(1)}, f32[48]{0:T(128)S(1)}) all-reduce(f32[48]{0:T(128)S(1)} %get-tuple-element.8, f32[48]{0:T(128)S(1)} %get-tuple-element.7), channel_id=1, replica_groups=mesh['wide'=16,'narrow'=2] {'wide','narrow'}, use_global_device_ids=true, to_apply=%region_37.38 | all-reduce | flops 96 | bytes 768 | tf_op jit(solution)/shard_map/psum | solution.py:69
  486.7 5.3 fusion.10
  492.0 40.2 %psum.173 = f32[256,48]{0,1:T(8,128)S(1)} all-reduce(f32[256,48]{0,1:T(8,128)S(1)} %fusion.10), channel_id=1, replica_groups=mesh['wide'=16,'narrow'=2] {'wide','narrow'}, use_global_device_ids=true, to_apply=%region_38.39 | all-reduce | flops 12288 | bytes 98304 | tf_op jit(solution)/shard_map/psum | solution.py:90
  532.2 7.3 %convolution_subtract_fusion.1 = f32[48,4096]{1,0:T(8,128)S(1)} fusion(f32[32,8,32,128]{3,2,1,0:T(8,128)} %bitcast.104, f32[6,8,32,128]{3,2,1,0:T(8,128)S(1)} %bitcast.111, f32[256,48]{0,1:T(8,128)S(1)} %psum.173), kind=kOutput, calls=%fused_computation.16 | convolution fusion | flops 604188672 | bytes 5816320 | tf_op jit(solution)/shard_map/bk,bc->kc/dot_general | solution.py:93
  539.6 5.3 fusion.13
  544.9 41.0 %psum.174 = f32[256,48]{0,1:T(8,128)S(1)} all-reduce(f32[256,48]{0,1:T(8,128)S(1)} %fusion.13), channel_id=1, replica_groups=mesh['wide'=16,'narrow'=2] {'wide','narrow'}, use_global_device_ids=true, to_apply=%region_39.40 | all-reduce | flops 12288 | bytes 98304 | tf_op jit(solution)/shard_map/psum | solution.py:95
  586.6 7.0 %multiply_reduce_fusion = (f32[48]{0:T(128)S(1)}, f32[48,4096]{1,0:T(8,128)S(1)}) fusion(f32[48,4096]{1,0:T(8,128)S(1)} %convolution_subtract_fusion.1, f32[32,8,32,128]{3,2,1,0:T(8,128)} %bitcast.105, f32[256,48]{0,1:T(8,128)S(1)} %psum.174), kind=kOutput, calls=%fused_computation.211 | convolution fusion | flops 604581824 | bytes 5816512 | tf_op jit(solution)/shard_map/bk,bc->kc/dot_general | solution.py:98
  593.6 39.6 %psum.175 = f32[48]{0:T(128)S(1)} all-reduce(f32[48]{0:T(128)S(1)} %get-tuple-element.84), channel_id=1, replica_groups=mesh['wide'=16,'narrow'=2] {'wide','narrow'}, use_global_device_ids=true, to_apply=%region_41.42 | all-reduce | flops 48 | bytes 384 | tf_op jit(solution)/shard_map/psum | solution.py:99
  (127 shorter events, 89.3 us)
Async XLA Ops:
  1.9 9.0 %collective-permute-start.1 = (f32[48,1,8,128]{3,0,2,1:T(8,128)S(1)}, f32[48,1,8,128]{3,0,2,1:T(8,128)S(1)}, u32[]{:S(2)}, u32[]{:S(2)}) collective-permute-start(f32[48,1,8,128]{3,0,2,1:T(8,128)S(1)} %get-tuple-element.82), channel_id=1, source_target_pairs={{0,2},{2,4},{4,6},{6,8},{8,10},{10,12},{12,14},{14,16},{16,18},{18... | collective-permute-start | bytes 589832 | tf_op jit(solution)/shard_map/ppermute | solution.py:17
  6.8 10.3 %collective-permute-start = (f32[48,1,8,128]{3,0,2,1:T(8,128)S(1)}, f32[48,1,8,128]{3,0,2,1:T(8,128)S(1)}, u32[]{:S(2)}, u32[]{:S(2)}) collective-permute-start(f32[48,1,8,128]{3,0,2,1:T(8,128)S(1)} %get-tuple-element.83), channel_id=1, source_target_pairs={{2,0},{4,2},{6,4},{8,6},{10,8},{12,10},{14,12},{16,14},{18,16},{20... | collective-permute-start | bytes 589832 | tf_op jit(solution)/shard_map/ppermute | solution.py:19
  17.1 3.1 collective-permute-start.3
  18.4 3.3 collective-permute-start.2
  63.5 11.6 %collective-permute-start.5 = (f32[48,1,8,128]{3,0,2,1:T(8,128)S(1)}, f32[48,1,8,128]{3,0,2,1:T(8,128)S(1)}, u32[]{:S(2)}, u32[]{:S(2)}) collective-permute-start(f32[48,1,8,128]{3,0,2,1:T(8,128)S(1)} %get-tuple-element.80), channel_id=1, source_target_pairs={{0,2},{2,4},{4,6},{6,8},{8,10},{10,12},{12,14},{14,16},{16,18},{18... | collective-permute-start | bytes 589832 | tf_op jit(solution)/shard_map/ppermute | solution.py:17
  67.7 9.3 %collective-permute-start.4 = (f32[48,1,8,128]{3,0,2,1:T(8,128)S(1)}, f32[48,1,8,128]{3,0,2,1:T(8,128)S(1)}, u32[]{:S(2)}, u32[]{:S(2)}) collective-permute-start(f32[48,1,8,128]{3,0,2,1:T(8,128)S(1)} %get-tuple-element.81), channel_id=1, source_target_pairs={{2,0},{4,2},{6,4},{8,6},{10,8},{12,10},{14,12},{16,14},{18,16},{20... | collective-permute-start | bytes 589832 | tf_op jit(solution)/shard_map/ppermute | solution.py:19
  77.0 2.6 collective-permute-start.7
  78.3 3.3 collective-permute-start.6
  122.9 11.6 %collective-permute-start.9 = (f32[48,1,8,128]{3,0,2,1:T(8,128)S(1)}, f32[48,1,8,128]{3,0,2,1:T(8,128)S(1)}, u32[]{:S(2)}, u32[]{:S(2)}) collective-permute-start(f32[48,1,8,128]{3,0,2,1:T(8,128)S(1)} %get-tuple-element.78), channel_id=1, source_target_pairs={{0,2},{2,4},{4,6},{6,8},{8,10},{10,12},{12,14},{14,16},{16,18},{18... | collective-permute-start | bytes 589832 | tf_op jit(solution)/shard_map/ppermute | solution.py:17
  127.1 9.3 %collective-permute-start.8 = (f32[48,1,8,128]{3,0,2,1:T(8,128)S(1)}, f32[48,1,8,128]{3,0,2,1:T(8,128)S(1)}, u32[]{:S(2)}, u32[]{:S(2)}) collective-permute-start(f32[48,1,8,128]{3,0,2,1:T(8,128)S(1)} %get-tuple-element.79), channel_id=1, source_target_pairs={{2,0},{4,2},{6,4},{8,6},{10,8},{12,10},{14,12},{16,14},{18,16},{20... | collective-permute-start | bytes 589832 | tf_op jit(solution)/shard_map/ppermute | solution.py:19
  136.4 2.6 collective-permute-start.11
  137.7 3.3 collective-permute-start.10
  182.2 7.4 %collective-permute-start.13 = (f32[48,1,8,128]{3,0,2,1:T(8,128)S(1)}, f32[48,1,8,128]{3,0,2,1:T(8,128)S(1)}, u32[]{:S(2)}, u32[]{:S(2)}) collective-permute-start(f32[48,1,8,128]{3,0,2,1:T(8,128)S(1)} %get-tuple-element.76), channel_id=1, source_target_pairs={{0,2},{2,4},{4,6},{6,8},{8,10},{10,12},{12,14},{14,16},{16,18},{18... | collective-permute-start | bytes 589832 | tf_op jit(solution)/shard_map/ppermute | solution.py:17
  186.4 9.1 %collective-permute-start.12 = (f32[48,1,8,128]{3,0,2,1:T(8,128)S(1)}, f32[48,1,8,128]{3,0,2,1:T(8,128)S(1)}, u32[]{:S(2)}, u32[]{:S(2)}) collective-permute-start(f32[48,1,8,128]{3,0,2,1:T(8,128)S(1)} %get-tuple-element.77), channel_id=1, source_target_pairs={{2,0},{4,2},{6,4},{8,6},{10,8},{12,10},{14,12},{16,14},{18,16},{20... | collective-permute-start | bytes 589832 | tf_op jit(solution)/shard_map/ppermute | solution.py:19
  195.5 2.6 collective-permute-start.15
  196.8 3.3 collective-permute-start.14
  243.3 11.6 %collective-permute-start.17 = (f32[48,1,8,128]{3,0,2,1:T(8,128)S(1)}, f32[48,1,8,128]{3,0,2,1:T(8,128)S(1)}, u32[]{:S(2)}, u32[]{:S(2)}) collective-permute-start(f32[48,1,8,128]{3,0,2,1:T(8,128)S(1)} %get-tuple-element.74), channel_id=1, source_target_pairs={{0,2},{2,4},{4,6},{6,8},{8,10},{10,12},{12,14},{14,16},{16,18},{18... | collective-permute-start | bytes 589832 | tf_op jit(solution)/shard_map/ppermute | solution.py:17
  247.5 9.3 %collective-permute-start.16 = (f32[48,1,8,128]{3,0,2,1:T(8,128)S(1)}, f32[48,1,8,128]{3,0,2,1:T(8,128)S(1)}, u32[]{:S(2)}, u32[]{:S(2)}) collective-permute-start(f32[48,1,8,128]{3,0,2,1:T(8,128)S(1)} %get-tuple-element.75), channel_id=1, source_target_pairs={{2,0},{4,2},{6,4},{8,6},{10,8},{12,10},{14,12},{16,14},{18,16},{20... | collective-permute-start | bytes 589832 | tf_op jit(solution)/shard_map/ppermute | solution.py:19
  256.8 2.8 collective-permute-start.19
  258.1 3.3 collective-permute-start.18
  303.6 7.4 %collective-permute-start.21 = (f32[48,1,8,128]{3,0,2,1:T(8,128)S(1)}, f32[48,1,8,128]{3,0,2,1:T(8,128)S(1)}, u32[]{:S(2)}, u32[]{:S(2)}) collective-permute-start(f32[48,1,8,128]{3,0,2,1:T(8,128)S(1)} %get-tuple-element.72), channel_id=1, source_target_pairs={{0,2},{2,4},{4,6},{6,8},{8,10},{10,12},{12,14},{14,16},{16,18},{18... | collective-permute-start | bytes 589832 | tf_op jit(solution)/shard_map/ppermute | solution.py:17
  307.8 9.1 %collective-permute-start.20 = (f32[48,1,8,128]{3,0,2,1:T(8,128)S(1)}, f32[48,1,8,128]{3,0,2,1:T(8,128)S(1)}, u32[]{:S(2)}, u32[]{:S(2)}) collective-permute-start(f32[48,1,8,128]{3,0,2,1:T(8,128)S(1)} %get-tuple-element.73), channel_id=1, source_target_pairs={{2,0},{4,2},{6,4},{8,6},{10,8},{12,10},{14,12},{16,14},{18,16},{20... | collective-permute-start | bytes 589832 | tf_op jit(solution)/shard_map/ppermute | solution.py:19
  316.9 2.6 collective-permute-start.23
  318.2 3.3 collective-permute-start.22
  364.9 11.6 %collective-permute-start.25 = (f32[48,1,8,128]{3,0,2,1:T(8,128)S(1)}, f32[48,1,8,128]{3,0,2,1:T(8,128)S(1)}, u32[]{:S(2)}, u32[]{:S(2)}) collective-permute-start(f32[48,1,8,128]{3,0,2,1:T(8,128)S(1)} %get-tuple-element.70), channel_id=1, source_target_pairs={{0,2},{2,4},{4,6},{6,8},{8,10},{10,12},{12,14},{14,16},{16,18},{18... | collective-permute-start | bytes 589832 | tf_op jit(solution)/shard_map/ppermute | solution.py:17
  369.1 9.3 %collective-permute-start.24 = (f32[48,1,8,128]{3,0,2,1:T(8,128)S(1)}, f32[48,1,8,128]{3,0,2,1:T(8,128)S(1)}, u32[]{:S(2)}, u32[]{:S(2)}) collective-permute-start(f32[48,1,8,128]{3,0,2,1:T(8,128)S(1)} %get-tuple-element.71), channel_id=1, source_target_pairs={{2,0},{4,2},{6,4},{8,6},{10,8},{12,10},{14,12},{16,14},{18,16},{20... | collective-permute-start | bytes 589832 | tf_op jit(solution)/shard_map/ppermute | solution.py:19
  378.4 2.6 collective-permute-start.27
  379.7 3.3 collective-permute-start.26
  425.2 7.4 %collective-permute-start.29 = (f32[48,1,8,128]{3,0,2,1:T(8,128)S(1)}, f32[48,1,8,128]{3,0,2,1:T(8,128)S(1)}, u32[]{:S(2)}, u32[]{:S(2)}) collective-permute-start(f32[48,1,8,128]{3,0,2,1:T(8,128)S(1)} %get-tuple-element.68), channel_id=1, source_target_pairs={{0,2},{2,4},{4,6},{6,8},{8,10},{10,12},{12,14},{14,16},{16,18},{18... | collective-permute-start | bytes 589832 | tf_op jit(solution)/shard_map/ppermute | solution.py:17
  429.4 9.1 %collective-permute-start.28 = (f32[48,1,8,128]{3,0,2,1:T(8,128)S(1)}, f32[48,1,8,128]{3,0,2,1:T(8,128)S(1)}, u32[]{:S(2)}, u32[]{:S(2)}) collective-permute-start(f32[48,1,8,128]{3,0,2,1:T(8,128)S(1)} %get-tuple-element.69), channel_id=1, source_target_pairs={{2,0},{4,2},{6,4},{8,6},{10,8},{12,10},{14,12},{16,14},{18,16},{20... | collective-permute-start | bytes 589832 | tf_op jit(solution)/shard_map/ppermute | solution.py:19
  438.5 2.6 collective-permute-start.31
  439.8 3.3 collective-permute-start.30
  (10 other events, 309.1 us)
where the time goes:
time: 646 us; the launch traced here: 635 us
  blocking collectives  433 us (67%)
  waiting for transfers between devices  79.2 us (12%)
  starting transfers between devices  65.5 us (10%)
  other arithmetic  26.5 us (4%)
  matrix products  25 us (4%)
    psum x4, blocking collectives, shards(): lax.psum((local_dot(halfway_image, halfway), local_dot(halfway_image, hal...  157 us
    psum x4, blocking collectives, shards(): lax.psum(local_dot(shadow, search_image), ('wide', 'narrow')) / total_cells  155 us
    ppermute x16, waiting for transfers between devices, padded_2(): lax.ppermute(head, axis, [((i + 1) % count, i) for i in range(ends)])  46.5 us
    ppermute x16, starting transfers between devices, padded_2(): lax.ppermute(tail, axis, [(i, (i + 1) % count) for i in range(ends)])  44.6 us
    psum x1, blocking collectives, shards(): lax.psum(jnp.einsum('bc,kc->bk', vflat, once, precision=high), ('wide', '...  41 us
    psum x1, blocking collectives, shards(): lax.psum(jnp.einsum('bc,kc->bk', vflat, wflat, precision=high), ('wide',...  40.2 us
    psum x1, blocking collectives, shards(): lax.psum(jnp.sum(twice * twice, axis=1), ('wide', 'narrow')) / total_cells  39.6 us
    ppermute x16, waiting for transfers between devices, padded_2(): lax.ppermute(tail, axis, [(i, (i + 1) % count) for i in range(ends)])  32.8 us
  transfers between devices with their start and end apart: 32, of which 24 were waited for; matrix products, arithmetic and copies ran while one was open for 0% of the time, Pallas kernels for 0%

commit v1 on v0

--- a/solution.py
+++ b/solution.py
@@ -87,7 +87,12 @@
     wflat = solution.reshape(columns, -1)
     high = lax.Precision.HIGHEST
     first_coef = (
-        lax.psum(jnp.einsum("bc,kc->bk", vflat, wflat, precision=high), ("wide", "narrow"))
+        jnp.sum(
+            lax.all_gather(
+                jnp.einsum("bc,kc->bk", vflat, wflat, precision=high), ("wide", "narrow")
+            ),
+            axis=0,
+        )
         / total_cells
     )
     once = wflat - jnp.einsum("bk,bc->kc", first_coef, vflat, precision=high)

time: 646 us -> 673 us (1.042)
  waiting for transfers between devices: 79.2 us -> 131 us
  blocking collectives: 433 us -> 392 us
  between operations: 1.79 us -> 15 us
    all_gather x0 -> x1, waiting for transfers between devices: none -> 52.1 us  [shards(): lax.all_gather(jnp.einsum('bc,kc->bk', vflat, wflat, precision=high), ('w...]
    psum x1 -> x0, blocking collectives: 40.2 us -> none  [shards(): lax.psum(jnp.einsum('bc,kc->bk', vflat, wflat, precision=high), ('wide',...]
  transfers between devices with their start and end apart: 32 -> 33, of which waited for: 24 -> 25; matrix products, arithmetic and copies ran while one was open for 0% -> 0% of each run, Pallas kernels for 0% -> 0%
where the time goes in v1:
time: 673 us; the launch traced here: 662 us
  blocking collectives  392 us (58%)
  waiting for transfers between devices  131 us (19%)
  starting transfers between devices  65.8 us (10%)
  other arithmetic  26.7 us (4%)
  matrix products  23.6 us (4%)
  between operations  15 us (2%)
  local copies, waits for them, and re-layouts  7.49 us (1%)
    psum x4, blocking collectives, shards(): lax.psum((local_dot(halfway_image, halfway), local_dot(halfway_image, hal...  157 us
    psum x4, blocking collectives, shards(): lax.psum(local_dot(shadow, search_image), ('wide', 'narrow')) / total_cells  155 us
    all_gather x1, waiting for transfers between devices, shards(): lax.all_gather(jnp.einsum('bc,kc->bk', vflat, wflat, precision=high), ('w...  52.1 us
    ppermute x16, waiting for transfers between devices, padded_2(): lax.ppermute(head, axis, [((i + 1) % count, i) for i in range(ends)])  46.2 us
    ppermute x16, starting transfers between devices, padded_2(): lax.ppermute(tail, axis, [(i, (i + 1) % count) for i in range(ends)])  44.6 us
    psum x1, blocking collectives, shards(): lax.psum(jnp.einsum('bc,kc->bk', vflat, once, precision=high), ('wide', '...  40.2 us
    psum x1, blocking collectives, shards(): lax.psum(jnp.sum(twice * twice, axis=1), ('wide', 'narrow')) / total_cells  39.1 us
    ppermute x16, waiting for transfers between devices, padded_2(): lax.ppermute(tail, axis, [(i, (i + 1) % count) for i in range(ends)])  32.7 us
  transfers between devices with their start and end apart: 33, of which 25 were waited for; matrix products, arithmetic and copies ran while one was open for 0% of the time, Pallas kernels for 0%

profile of v1, /device:TPU:0, one launch (start us, length us, event | category | flops | bytes accessed | tf_op | source)
XLA Modules:
  0.0 661.8 jit_solution(8546289106400398968)
XLA Ops:
  8.5 4.9 collective-permute-start.1
  14.7 2.8 collective-permute-done.1
  17.5 6.2 collective-permute-done
  29.6 40.2 %all-reduce.12 = (f32[48]{0:T(128)S(1)}, f32[48]{0:T(128)S(1)}) all-reduce(f32[48]{0:T(128)S(1)} %get-tuple-element.50, f32[48]{0:T(128)S(1)} %reduce_sum.192), channel_id=1, replica_groups=mesh['wide'=16,'narrow'=2] {'wide','narrow'}, use_global_device_ids=true, to_apply=%region_3.4 | all-reduce | flops 96 | bytes 768 | tf_op jit(solution)/shard_map/psum | solution.py:65
  70.1 4.2 collective-permute-start.5
  75.6 6.1 collective-permute-done.5
  89.8 39.4 %all-reduce.11 = (f32[48]{0:T(128)S(1)}, f32[48]{0:T(128)S(1)}, f32[48]{0:T(128)S(1)}, f32[48]{0:T(128)S(1)}) all-reduce(f32[48]{0:T(128)S(1)} %get-tuple-element.4, f32[48]{0:T(128)S(1)} %get-tuple-element.6, f32[48]{0:T(128)S(1)} %get-tuple-element.5, ...), channel_id=1, replica_groups=mesh['wide'=16,'narrow'=2] {'wide','narrow'}, use_global_device_ids=true, to_apply=%region_5.6 | all-reduce | flops 192 | bytes 1536 | tf_op jit(solution)/shard_map/psum | solution.py:69
  129.5 4.2 collective-permute-start.9
  135.0 6.1 collective-permute-done.9
  148.9 38.4 %psum.153 = f32[48]{0:T(128)S(1)} all-reduce(f32[48]{0:T(128)S(1)} %get-tuple-element.44), channel_id=1, replica_groups=mesh['wide'=16,'narrow'=2] {'wide','narrow'}, use_global_device_ids=true, to_apply=%region_13.14 | all-reduce | flops 48 | bytes 384 | tf_op jit(solution)/shard_map/psum | solution.py:65
  188.7 4.2 collective-permute-start.13
  196.1 5.9 collective-permute-done.12
  209.1 39.3 %all-reduce.10 = (f32[48]{0:T(128)S(1)}, f32[48]{0:T(128)S(1)}, f32[48]{0:T(128)S(1)}, f32[48]{0:T(128)S(1)}) all-reduce(f32[48]{0:T(128)S(1)} %get-tuple-element.14, f32[48]{0:T(128)S(1)} %get-tuple-element.16, f32[48]{0:T(128)S(1)} %get-tuple-element.15, ...), channel_id=1, replica_groups=mesh['wide'=16,'narrow'=2] {'wide','narrow'}, use_global_device_ids=true, to_apply=%region_15.16 | all-reduce | flops 192 | bytes 1536 | tf_op jit(solution)/shard_map/psum | solution.py:69
  249.8 4.2 collective-permute-start.17
  255.3 6.1 collective-permute-done.17
  270.1 38.4 %psum.158 = f32[48]{0:T(128)S(1)} all-reduce(f32[48]{0:T(128)S(1)} %get-tuple-element.38), channel_id=1, replica_groups=mesh['wide'=16,'narrow'=2] {'wide','narrow'}, use_global_device_ids=true, to_apply=%region_23.24 | all-reduce | flops 48 | bytes 384 | tf_op jit(solution)/shard_map/psum | solution.py:65
  310.1 4.2 collective-permute-start.21
  317.5 5.9 collective-permute-done.20
  330.5 39.3 %all-reduce.9 = (f32[48]{0:T(128)S(1)}, f32[48]{0:T(128)S(1)}, f32[48]{0:T(128)S(1)}, f32[48]{0:T(128)S(1)}) all-reduce(f32[48]{0:T(128)S(1)} %get-tuple-element.10, f32[48]{0:T(128)S(1)} %get-tuple-element.12, f32[48]{0:T(128)S(1)} %get-tuple-element.11, ...), channel_id=1, replica_groups=mesh['wide'=16,'narrow'=2] {'wide','narrow'}, use_global_device_ids=true, to_apply=%region_25.26 | all-reduce | flops 192 | bytes 1536 | tf_op jit(solution)/shard_map/psum | solution.py:69
  371.4 4.2 collective-permute-start.25
  376.9 6.1 collective-permute-done.25
  391.8 38.4 %psum.163 = f32[48]{0:T(128)S(1)} all-reduce(f32[48]{0:T(128)S(1)} %get-tuple-element.33), channel_id=1, replica_groups=mesh['wide'=16,'narrow'=2] {'wide','narrow'}, use_global_device_ids=true, to_apply=%region_33.34 | all-reduce | flops 48 | bytes 384 | tf_op jit(solution)/shard_map/psum | solution.py:65
  431.7 4.2 collective-permute-start.29
  439.1 5.9 collective-permute-done.28
  451.0 39.4 %all-reduce.8 = (f32[48]{0:T(128)S(1)}, f32[48]{0:T(128)S(1)}) all-reduce(f32[48]{0:T(128)S(1)} %get-tuple-element.8, f32[48]{0:T(128)S(1)} %get-tuple-element.7), channel_id=1, replica_groups=mesh['wide'=16,'narrow'=2] {'wide','narrow'}, use_global_device_ids=true, to_apply=%region_37.38 | all-reduce | flops 96 | bytes 768 | tf_op jit(solution)/shard_map/psum | solution.py:69
  493.7 6.0 fusion.10
  501.0 52.1 %all-gather.3.cloned.1.call-done = f32[8192,48]{0,1:T(8,128)} async-done(((f32[256,48]{0,1:T(8,128)}), f32[8192,48]{0,1:T(8,128)}) %all-gather.3.cloned.1.call-update) | async-done | bytes 1572880 | tf_op jit(solution)/shard_map/all_gather | solution.py:91
  555.8 5.1 convolution_subtract_fusion.1
  561.0 5.6 fusion.13
  566.5 40.2 %psum.166 = f32[256,48]{0,1:T(8,128)S(1)} all-reduce(f32[256,48]{0,1:T(8,128)S(1)} %fusion.13), channel_id=1, replica_groups=mesh['wide'=16,'narrow'=2] {'wide','narrow'}, use_global_device_ids=true, to_apply=%region_39.40 | all-reduce | flops 12288 | bytes 98304 | tf_op jit(solution)/shard_map/psum | solution.py:100
  607.4 7.0 %multiply_reduce_fusion = (f32[48]{0:T(128)S(1)}, f32[48,4096]{1,0:T(8,128)S(1)}) fusion(f32[48,4096]{1,0:T(8,128)S(1)} %convolution_subtract_fusion.1, f32[32,8,32,128]{3,2,1,0:T(8,128)} %bitcast.109, f32[256,48]{0,1:T(8,128)S(1)} %psum.166), kind=kOutput, calls=%fused_computation.212 | convolution fusion | flops 604581824 | bytes 5816512 | tf_op jit(solution)/shard_map/bk,bc->kc/dot_general | solution.py:103
  614.4 39.1 %psum.167 = f32[48]{0:T(128)S(1)} all-reduce(f32[48]{0:T(128)S(1)} %get-tuple-element.84), channel_id=1, replica_groups=mesh['wide'=16,'narrow'=2] {'wide','narrow'}, use_global_device_ids=true, to_apply=%region_41.42 | all-reduce | flops 48 | bytes 384 | tf_op jit(solution)/shard_map/psum | solution.py:104
  (133 shorter events, 93.6 us)
Async XLA Ops:
  7.2 546.0 %all-gather.3.cloned.1.call-start = ((), (), s32[]{:S(2)}) async-start(), calls=%async_computation | async-start | bytes 1622016 | tf_op jit(solution)/shard_map/all_gather | solution.py:91
  8.5 9.0 %collective-permute-start.1 = (f32[48,1,8,128]{3,0,2,1:T(8,128)S(1)}, f32[48,1,8,128]{3,0,2,1:T(8,128)S(1)}, u32[]{:S(2)}, u32[]{:S(2)}) collective-permute-start(f32[48,1,8,128]{3,0,2,1:T(8,128)S(1)} %get-tuple-element.82), channel_id=1, source_target_pairs={{0,2},{2,4},{4,6},{6,8},{8,10},{10,12},{12,14},{14,16},{16,18},{18... | collective-permute-start | bytes 589832 | tf_op jit(solution)/shard_map/ppermute | solution.py:17
  13.4 10.3 %collective-permute-start = (f32[48,1,8,128]{3,0,2,1:T(8,128)S(1)}, f32[48,1,8,128]{3,0,2,1:T(8,128)S(1)}, u32[]{:S(2)}, u32[]{:S(2)}) collective-permute-start(f32[48,1,8,128]{3,0,2,1:T(8,128)S(1)} %get-tuple-element.83), channel_id=1, source_target_pairs={{2,0},{4,2},{6,4},{8,6},{10,8},{12,10},{14,12},{16,14},{18,16},{20... | collective-permute-start | bytes 589832 | tf_op jit(solution)/shard_map/ppermute | solution.py:19
  23.7 3.1 collective-permute-start.3
  25.0 3.3 collective-permute-start.2
  70.1 11.6 %collective-permute-start.5 = (f32[48,1,8,128]{3,0,2,1:T(8,128)S(1)}, f32[48,1,8,128]{3,0,2,1:T(8,128)S(1)}, u32[]{:S(2)}, u32[]{:S(2)}) collective-permute-start(f32[48,1,8,128]{3,0,2,1:T(8,128)S(1)} %get-tuple-element.80), channel_id=1, source_target_pairs={{0,2},{2,4},{4,6},{6,8},{8,10},{10,12},{12,14},{14,16},{16,18},{18... | collective-permute-start | bytes 589832 | tf_op jit(solution)/shard_map/ppermute | solution.py:17
  74.3 9.3 %collective-permute-start.4 = (f32[48,1,8,128]{3,0,2,1:T(8,128)S(1)}, f32[48,1,8,128]{3,0,2,1:T(8,128)S(1)}, u32[]{:S(2)}, u32[]{:S(2)}) collective-permute-start(f32[48,1,8,128]{3,0,2,1:T(8,128)S(1)} %get-tuple-element.81), channel_id=1, source_target_pairs={{2,0},{4,2},{6,4},{8,6},{10,8},{12,10},{14,12},{16,14},{18,16},{20... | collective-permute-start | bytes 589832 | tf_op jit(solution)/shard_map/ppermute | solution.py:19
  83.6 2.6 collective-permute-start.7
  84.9 3.3 collective-permute-start.6
  129.5 11.6 %collective-permute-start.9 = (f32[48,1,8,128]{3,0,2,1:T(8,128)S(1)}, f32[48,1,8,128]{3,0,2,1:T(8,128)S(1)}, u32[]{:S(2)}, u32[]{:S(2)}) collective-permute-start(f32[48,1,8,128]{3,0,2,1:T(8,128)S(1)} %get-tuple-element.78), channel_id=1, source_target_pairs={{0,2},{2,4},{4,6},{6,8},{8,10},{10,12},{12,14},{14,16},{16,18},{18... | collective-permute-start | bytes 589832 | tf_op jit(solution)/shard_map/ppermute | solution.py:17
  133.7 9.3 %collective-permute-start.8 = (f32[48,1,8,128]{3,0,2,1:T(8,128)S(1)}, f32[48,1,8,128]{3,0,2,1:T(8,128)S(1)}, u32[]{:S(2)}, u32[]{:S(2)}) collective-permute-start(f32[48,1,8,128]{3,0,2,1:T(8,128)S(1)} %get-tuple-element.79), channel_id=1, source_target_pairs={{2,0},{4,2},{6,4},{8,6},{10,8},{12,10},{14,12},{16,14},{18,16},{20... | collective-permute-start | bytes 589832 | tf_op jit(solution)/shard_map/ppermute | solution.py:19
  143.0 2.6 collective-permute-start.11
  144.3 3.3 collective-permute-start.10
  188.7 7.4 %collective-permute-start.13 = (f32[48,1,8,128]{3,0,2,1:T(8,128)S(1)}, f32[48,1,8,128]{3,0,2,1:T(8,128)S(1)}, u32[]{:S(2)}, u32[]{:S(2)}) collective-permute-start(f32[48,1,8,128]{3,0,2,1:T(8,128)S(1)} %get-tuple-element.76), channel_id=1, source_target_pairs={{0,2},{2,4},{4,6},{6,8},{8,10},{10,12},{12,14},{14,16},{16,18},{18... | collective-permute-start | bytes 589832 | tf_op jit(solution)/shard_map/ppermute | solution.py:17
  192.9 9.1 %collective-permute-start.12 = (f32[48,1,8,128]{3,0,2,1:T(8,128)S(1)}, f32[48,1,8,128]{3,0,2,1:T(8,128)S(1)}, u32[]{:S(2)}, u32[]{:S(2)}) collective-permute-start(f32[48,1,8,128]{3,0,2,1:T(8,128)S(1)} %get-tuple-element.77), channel_id=1, source_target_pairs={{2,0},{4,2},{6,4},{8,6},{10,8},{12,10},{14,12},{16,14},{18,16},{20... | collective-permute-start | bytes 589832 | tf_op jit(solution)/shard_map/ppermute | solution.py:19
  202.0 2.6 collective-permute-start.15
  203.3 3.3 collective-permute-start.14
  249.8 11.6 %collective-permute-start.17 = (f32[48,1,8,128]{3,0,2,1:T(8,128)S(1)}, f32[48,1,8,128]{3,0,2,1:T(8,128)S(1)}, u32[]{:S(2)}, u32[]{:S(2)}) collective-permute-start(f32[48,1,8,128]{3,0,2,1:T(8,128)S(1)} %get-tuple-element.74), channel_id=1, source_target_pairs={{0,2},{2,4},{4,6},{6,8},{8,10},{10,12},{12,14},{14,16},{16,18},{18... | collective-permute-start | bytes 589832 | tf_op jit(solution)/shard_map/ppermute | solution.py:17
  254.0 9.3 %collective-permute-start.16 = (f32[48,1,8,128]{3,0,2,1:T(8,128)S(1)}, f32[48,1,8,128]{3,0,2,1:T(8,128)S(1)}, u32[]{:S(2)}, u32[]{:S(2)}) collective-permute-start(f32[48,1,8,128]{3,0,2,1:T(8,128)S(1)} %get-tuple-element.75), channel_id=1, source_target_pairs={{2,0},{4,2},{6,4},{8,6},{10,8},{12,10},{14,12},{16,14},{18,16},{20... | collective-permute-start | bytes 589832 | tf_op jit(solution)/shard_map/ppermute | solution.py:19
  263.3 3.1 collective-permute-start.19
  264.6 3.3 collective-permute-start.18
  310.1 7.4 %collective-permute-start.21 = (f32[48,1,8,128]{3,0,2,1:T(8,128)S(1)}, f32[48,1,8,128]{3,0,2,1:T(8,128)S(1)}, u32[]{:S(2)}, u32[]{:S(2)}) collective-permute-start(f32[48,1,8,128]{3,0,2,1:T(8,128)S(1)} %get-tuple-element.72), channel_id=1, source_target_pairs={{0,2},{2,4},{4,6},{6,8},{8,10},{10,12},{12,14},{14,16},{16,18},{18... | collective-permute-start | bytes 589832 | tf_op jit(solution)/shard_map/ppermute | solution.py:17
  314.3 9.1 %collective-permute-start.20 = (f32[48,1,8,128]{3,0,2,1:T(8,128)S(1)}, f32[48,1,8,128]{3,0,2,1:T(8,128)S(1)}, u32[]{:S(2)}, u32[]{:S(2)}) collective-permute-start(f32[48,1,8,128]{3,0,2,1:T(8,128)S(1)} %get-tuple-element.73), channel_id=1, source_target_pairs={{2,0},{4,2},{6,4},{8,6},{10,8},{12,10},{14,12},{16,14},{18,16},{20... | collective-permute-start | bytes 589832 | tf_op jit(solution)/shard_map/ppermute | solution.py:19
  323.4 2.6 collective-permute-start.23
  324.7 3.3 collective-permute-start.22
  371.4 11.6 %collective-permute-start.25 = (f32[48,1,8,128]{3,0,2,1:T(8,128)S(1)}, f32[48,1,8,128]{3,0,2,1:T(8,128)S(1)}, u32[]{:S(2)}, u32[]{:S(2)}) collective-permute-start(f32[48,1,8,128]{3,0,2,1:T(8,128)S(1)} %get-tuple-element.70), channel_id=1, source_target_pairs={{0,2},{2,4},{4,6},{6,8},{8,10},{10,12},{12,14},{14,16},{16,18},{18... | collective-permute-start | bytes 589832 | tf_op jit(solution)/shard_map/ppermute | solution.py:17
  375.6 9.3 %collective-permute-start.24 = (f32[48,1,8,128]{3,0,2,1:T(8,128)S(1)}, f32[48,1,8,128]{3,0,2,1:T(8,128)S(1)}, u32[]{:S(2)}, u32[]{:S(2)}) collective-permute-start(f32[48,1,8,128]{3,0,2,1:T(8,128)S(1)} %get-tuple-element.71), channel_id=1, source_target_pairs={{2,0},{4,2},{6,4},{8,6},{10,8},{12,10},{14,12},{16,14},{18,16},{20... | collective-permute-start | bytes 589832 | tf_op jit(solution)/shard_map/ppermute | solution.py:19
  385.0 2.6 collective-permute-start.27
  386.3 3.3 collective-permute-start.26
  431.7 7.4 %collective-permute-start.29 = (f32[48,1,8,128]{3,0,2,1:T(8,128)S(1)}, f32[48,1,8,128]{3,0,2,1:T(8,128)S(1)}, u32[]{:S(2)}, u32[]{:S(2)}) collective-permute-start(f32[48,1,8,128]{3,0,2,1:T(8,128)S(1)} %get-tuple-element.68), channel_id=1, source_target_pairs={{0,2},{2,4},{4,6},{6,8},{8,10},{10,12},{12,14},{14,16},{16,18},{18... | collective-permute-start | bytes 589832 | tf_op jit(solution)/shard_map/ppermute | solution.py:17
  435.9 9.1 %collective-permute-start.28 = (f32[48,1,8,128]{3,0,2,1:T(8,128)S(1)}, f32[48,1,8,128]{3,0,2,1:T(8,128)S(1)}, u32[]{:S(2)}, u32[]{:S(2)}) collective-permute-start(f32[48,1,8,128]{3,0,2,1:T(8,128)S(1)} %get-tuple-element.69), channel_id=1, source_target_pairs={{2,0},{4,2},{6,4},{8,6},{10,8},{12,10},{14,12},{16,14},{18,16},{20... | collective-permute-start | bytes 589832 | tf_op jit(solution)/shard_map/ppermute | solution.py:19
  446.4 3.3 collective-permute-start.30
  (12 other events, 308.2 us)
Sparse Core Ops, SparseCore 0:
  499.8 53.3 all-gather.2
